TPU v7x, 32 devices: a whole 2x2x4 slice. The times are simulated.
32 devices in a mesh: bank: 4 (over z), zero: 8 (over y, x, core).
Axes of the slice: x: 2, y: 2, z: 4, core: 2. Of those that a mesh axis runs over, the one named last changes fastest.
Arguments:
- master_gate: float32 [64, 2048, 1024], P('bank', 'zero'), may hold values from -0.1875 to 0.1875
- second_gate: bfloat16 [64, 2048, 1024], P('bank', 'zero'), may hold values from -0.0625 to 0.0625
- master_up: float32 [64, 2048, 1024], P('bank', 'zero'), may hold values from -0.1875 to 0.1875
- second_up: bfloat16 [64, 2048, 1024], P('bank', 'zero'), may hold values from -0.0625 to 0.0625
- master_down: float32 [64, 1024, 2048], P('bank', None, 'zero'), may hold values from -0.25 to 0.25
- second_down: bfloat16 [64, 1024, 2048], P('bank', None, 'zero'), may hold values from -0.09375 to 0.09375
- router_weight: float32 [2048, 64], P('zero', 'bank'), may hold values from -0.125 to 0.125
- router_gain: float32 [2048], P('zero'), may hold values from 0.25 to 1.75
Outputs:
- final_gate: bfloat16 [64, 2048, 1024], P('bank', None, 'zero')
- final_up: bfloat16 [64, 2048, 1024], P('bank', None, 'zero')
- final_down: bfloat16 [64, 1024, 2048], P('bank', 'zero')
- scale_gate: float32 [64, 1024], P('bank', 'zero')
- scale_up: float32 [64, 1024], P('bank', 'zero')
- scale_down: float32 [64, 1024], P('bank', 'zero')
- serve_router: bfloat16 [2048, 64], replicated
All inputs are finite; a program needn't handle non-finite values. Where the computation divides by a largest or mean magnitude, that divisor is 1e-20 or more.
Results may differ from a plain program's by a relative error of at most 0.001.
Values may be sent and summed in bfloat16 or wider, within the bound.
No kernel may reach another device: no remote copies, remote signals or barrier semaphores. Data moves between devices by JAX's collectives and lax.ppermute only.
A program may use at most 192 MiB of HBM per device.

v0:
```python
import jax
import jax.numpy as jnp
from jax import lax
from jax.sharding import PartitionSpec as P

D_MODEL = 2048


def on_device(
    master_gate,
    second_gate,
    master_up,
    second_up,
    master_down,
    second_down,
    router_weight,
    router_gain,
):
    merged_gate = master_gate + second_gate.astype(jnp.float32)
    merged_up = master_up + second_up.astype(jnp.float32)
    merged_down = master_down + second_down.astype(jnp.float32)
    total_gate, total_up, total_down = lax.psum(
        (
            jnp.sum(jnp.abs(merged_gate), axis=1),
            jnp.sum(jnp.abs(merged_up), axis=1),
            jnp.sum(jnp.abs(merged_down), axis=2),
        ),
        "zero",
    )
    scale_gate = total_gate / D_MODEL
    scale_up = total_up / D_MODEL
    scale_down = total_down / D_MODEL
    narrow_gate, narrow_up, narrow_down = (
        (merged_gate / jnp.expand_dims(scale_gate, 1)).astype(jnp.bfloat16),
        (merged_up / jnp.expand_dims(scale_up, 1)).astype(jnp.bfloat16),
        (merged_down / jnp.expand_dims(scale_down, 2)).astype(jnp.bfloat16),
    )
    final_gate, final_up = (
        lax.all_to_all(narrow_gate, "zero", split_axis=2, concat_axis=1, tiled=True),
        lax.all_to_all(narrow_up, "zero", split_axis=2, concat_axis=1, tiled=True),
    )
    final_down = lax.all_to_all(narrow_down, "zero", split_axis=1, concat_axis=2, tiled=True)
    scale_gate = lax.dynamic_slice_in_dim(
        scale_gate, lax.axis_index("zero") * final_gate.shape[2], final_gate.shape[2], axis=1
    )
    scale_up = lax.dynamic_slice_in_dim(
        scale_up, lax.axis_index("zero") * final_up.shape[2], final_up.shape[2], axis=1
    )
    scale_down = lax.dynamic_slice_in_dim(
        scale_down, lax.axis_index("zero") * final_down.shape[1], final_down.shape[1], axis=1
    )
    part_router = (router_weight * router_gain[:, None]).astype(jnp.bfloat16)
    row_router = lax.all_gather(part_router, "zero", axis=0, tiled=True)
    serve_router = lax.all_gather(row_router, "bank", axis=1, tiled=True)
    return (final_gate, final_up, final_down, scale_gate, scale_up, scale_down, serve_router)


def solution(mesh):
    return jax.shard_map(
        on_device,
        mesh=mesh,
        in_specs=(
            P("bank", "zero", None),
            P("bank", "zero", None),
            P("bank", "zero", None),
            P("bank", "zero", None),
            P("bank", None, "zero"),
            P("bank", None, "zero"),
            P("zero", "bank"),
            P("zero"),
        ),
        out_specs=(
            P("bank", None, "zero"),
            P("bank", None, "zero"),
            P("bank", "zero", None),
            P("bank", "zero"),
            P("bank", "zero"),
            P("bank", "zero"),
            P(),
        ),
        check_vma=False,
    )
```

profile of v0, /device:TPU:0, one launch (start us, length us, event | category | flops | bytes accessed | tf_op | source)
XLA Modules:
  0.0 554.7 jit_solution(10408405090956699153)
XLA Ops:
  7.2 0.0 all-reduce.3.cloned.1.call-start
  7.2 17.6 %copy.31 = f32[16,256,1024]{1,0,2:T(8,128)} copy(f32[16,256,1024]{2,1,0:T(8,128)} %param.8) | data formatting | bytes 33554432 | tf_op args[0]
  24.8 17.6 %copy.34 = f32[16,256,1024]{1,0,2:T(8,128)} copy(f32[16,256,1024]{2,1,0:T(8,128)} %param.10) | data formatting | bytes 33554432 | tf_op args[2]
  42.4 12.5 %copy.30 = bf16[16,256,1024]{1,0,2:T(8,128)(2,1)} copy(bf16[16,256,1024]{2,1,0:T(8,128)(2,1)} %param.9) | data formatting | bytes 16777216 | tf_op args[1]
  54.9 12.5 %copy.33 = bf16[16,256,1024]{1,0,2:T(8,128)(2,1)} copy(bf16[16,256,1024]{2,1,0:T(8,128)(2,1)} %param.11) | data formatting | bytes 16777216 | tf_op args[3]
  67.4 0.0 copy-start
  67.4 0.0 copy-start.1
  67.4 25.3 %abs_reduce_fusion = f32[16,1024]{0,1:T(8,128)} fusion(f32[16,1024,256]{2,1,0:T(8,128)} %param.12, bf16[16,1024,256]{2,1,0:T(8,128)(2,1)} %param.13), kind=kLoop, calls=%fused_computation.2 | loop fusion | flops 16760832 | bytes 25231360 | tf_op jit(solution)/shard_map/reduce_sum | solution.py:26
  92.7 0.0 copy-done
  92.7 0.0 copy-done.1
  92.7 13.2 %abs_reduce_fusion.1 = (f32[16,1024]{0,1:T(8,128)}, f32[16,1024]{0,1:T(8,128)}) fusion(f32[16,256,1024]{1,0,2:T(8,128)} %copy.34, bf16[16,256,1024]{1,0,2:T(8,128)(2,1)S(1)} %copy-done.1, f32[16,256,1024]{1,0,2:T(8,128)} %copy.31, bf16[16,256,1024]{1,0,2:T(8,128)(2,1)S(1)} %copy-done), kind=kLoop, calls=%fused_computation.4 | loop fusion | flops 33521664 | bytes 50462720 | tf_op jit(solution)/shard_map/reduce_sum | solution.py:25
  105.9 0.0 all-reduce.3.cloned.1.call-update
  105.9 62.0 %all-reduce.3.cloned.1.call-done = (f32[16,1024]{0,1:T(8,128)}, f32[16,1024]{0,1:T(8,128)}, f32[16,1024]{0,1:T(8,128)}) async-done(((f32[16,1024]{0,1:T(8,128)}, f32[16,1024]{0,1:T(8,128)}, f32[16,1024]{0,1:T(8,128)}), (f32[16,1024]{0,1:T(8,128)}, f32[16,1024]{0,1:T(8,128)}, f32[16,1024]{0,1:T(8,128)})) %all-reduce.3.cloned.1.call-update) | async-done | bytes 196624 | tf_op jit(solution)/shard_map/psum | solution.py:22
  167.9 1.1 broadcast_multiply_fusion.1
  169.0 12.0 %divide_convert_fusion.1 = bf16[16,256,1024]{1,0,2:T(8,128)(2,1)} fusion(f32[16,256,1024]{1,0,2:T(8,128)} %copy.34, bf16[16,256,1024]{1,0,2:T(8,128)(2,1)} %copy.33, f32[16,1024]{0,1:T(8,128)S(1)} %broadcast_multiply_fusion.1), kind=kLoop, calls=%fused_computation.3 | loop fusion | flops 16777216 | bytes 33619968 | tf_op jit(solution)/shard_map/convert_element_type | solution.py:35
  180.9 0.0 copy-start.3
  180.9 5.1 all-to-all-start.1
  186.0 0.0 copy-done.3
  186.1 12.0 %divide_convert_fusion.2 = bf16[16,256,1024]{1,0,2:T(8,128)(2,1)} fusion(f32[16,256,1024]{1,0,2:T(8,128)} %copy.31, bf16[16,256,1024]{1,0,2:T(8,128)(2,1)} %copy.30, f32[16,1024]{0,1:T(8,128)S(1)} %broadcast_multiply_fusion.2), kind=kLoop, calls=%fused_computation.6 | loop fusion | flops 16777216 | bytes 33619968 | tf_op jit(solution)/shard_map/convert_element_type | solution.py:34
  198.1 0.0 copy-start.2
  198.1 82.0 %all-to-all-done.1 = bf16[16,256,1024]{1,0,2:T(8,128)(2,1)} async-done(((bf16[16,256,1024]{1,0,2:T(8,128)(2,1)}), bf16[16,256,1024]{1,0,2:T(8,128)(2,1)}, u32[]{:S(2)}, u32[]{:S(2)}) %all-to-all-start.1) | async-done | bytes 8388640 | tf_op jit(solution)/shard_map/all_to_all | solution.py:40
  280.1 5.1 all-to-all-start
  285.2 0.0 copy-done.2
  285.3 23.8 %divide_convert_fusion = bf16[16,1024,256]{2,0,1:T(8,128)(2,1)} fusion(f32[16,1024,256]{2,1,0:T(8,128)} %param.12, f32[16,1024]{0,1:T(8,128)S(1)} %broadcast_multiply_fusion, bf16[16,1024,256]{2,1,0:T(8,128)(2,1)} %param.13), kind=kLoop, calls=%fused_computation.1 | loop fusion | flops 16777216 | bytes 33619968 | tf_op jit(solution)/shard_map/convert_element_type | solution.py:36
  309.0 0.0 copy-start.4
  309.0 0.0 copy-start.5
  309.0 70.0 %all-to-all-done = bf16[16,256,1024]{1,0,2:T(8,128)(2,1)} async-done(((bf16[16,256,1024]{1,0,2:T(8,128)(2,1)}), bf16[16,256,1024]{1,0,2:T(8,128)(2,1)}, u32[]{:S(2)}, u32[]{:S(2)}) %all-to-all-start) | async-done | bytes 8388640 | tf_op jit(solution)/shard_map/all_to_all | solution.py:39
  379.1 5.0 all-to-all-start.2
  384.1 0.0 copy-done.4
  384.1 0.0 copy-done.5
  384.1 97.2 %all_gather.6 = bf16[2048,16]{0,1:T(8,128)(2,1)S(1)} all-gather(bf16[256,16]{0,1:T(8,128)(2,1)S(1)} %multiply_convert_fusion), channel_id=1, replica_groups=mesh['bank'=4,'zero'=8] {'zero'}, dimensions={0}, use_global_device_ids=true | all-gather | bytes 73728 | tf_op jit(solution)/shard_map/all_gather | solution.py:53
  481.3 14.4 %all_gather.7 = bf16[2048,64]{0,1:T(8,128)(2,1)S(1)} all-gather(bf16[2048,16]{0,1:T(8,128)(2,1)S(1)} %all_gather.6), channel_id=1, replica_groups=mesh['bank'=4,'zero'=8] {'bank'}, dimensions={1}, use_global_device_ids=true | all-gather | bytes 327680 | tf_op jit(solution)/shard_map/all_gather | solution.py:54
  495.7 0.7 copy.39
  496.4 0.7 copy.40
  497.1 0.7 copy.41
  497.8 12.3 %copy.35 = bf16[16,8,256,128]{3,2,1,0:T(8,128)(2,1)} copy(bf16[16,8,256,128]{2,0,3,1:T(8,128)(2,1)} %bitcast.4) | data formatting | bytes 16777216 | tf_op jit(solution)/shard_map/all_to_all | solution.py:40
  510.0 12.3 %copy.32 = bf16[16,8,256,128]{3,2,1,0:T(8,128)(2,1)} copy(bf16[16,8,256,128]{2,0,3,1:T(8,128)(2,1)} %bitcast.1) | data formatting | bytes 16777216 | tf_op jit(solution)/shard_map/all_to_all | solution.py:39
  522.3 0.0 all-to-all-done.2
  522.3 11.4 %copy.38 = bf16[16,128,8,256]{3,2,1,0:T(8,128)(2,1)} copy(bf16[16,128,8,256]{3,0,1,2:T(8,128)(2,1)} %bitcast.7) | data formatting | bytes 16777216 | tf_op jit(solution)/shard_map/all_to_all | solution.py:42
  533.7 13.4 %all_to_all.50 = bf16[16,128,2048]{2,1,0:T(8,128)(2,1)} reshape(bf16[16,128,8,256]{3,2,1,0:T(8,128)(2,1)} %copy.38) | data formatting | bytes 16777216 | tf_op jit(solution)/shard_map/all_to_all | solution.py:42
  547.1 0.7 copy.53
  (6 shorter events, 0.1 us)
Async XLA Ops:
  7.2 160.7 %all-reduce.3.cloned.1.call-start = ((), (), s32[]{:S(2)}) async-start(), calls=%async_computation.3 | async-start | bytes 3145728 | tf_op jit(solution)/shard_map/psum | solution.py:22
  67.4 25.3 %copy-start = (bf16[16,256,1024]{1,0,2:T(8,128)(2,1)S(1)}, bf16[16,256,1024]{1,0,2:T(8,128)(2,1)}, u32[]{:S(2)}) copy-start(bf16[16,256,1024]{1,0,2:T(8,128)(2,1)} %copy.30) | copy-start | bytes 25165828
  67.4 25.3 %copy-start.1 = (bf16[16,256,1024]{1,0,2:T(8,128)(2,1)S(1)}, bf16[16,256,1024]{1,0,2:T(8,128)(2,1)}, u32[]{:S(2)}) copy-start(bf16[16,256,1024]{1,0,2:T(8,128)(2,1)} %copy.33) | copy-start | bytes 25165828
  180.9 5.1 copy-start.3
  180.9 99.1 %all-to-all-start.1 = ((bf16[16,256,1024]{1,0,2:T(8,128)(2,1)}), bf16[16,256,1024]{1,0,2:T(8,128)(2,1)}, u32[]{:S(2)}, u32[]{:S(2)}) async-start(bf16[16,256,1024]{1,0,2:T(8,128)(2,1)} %divide_convert_fusion.1), calls=%async_computation.1 | async-start | bytes 16777216 | tf_op jit(solution)/shard_map/all_to_all | solution.py:40
  198.1 87.1 %copy-start.2 = (f32[16,1024]{0,1:T(8,128)S(1)}, f32[16,1024]{0,1:T(8,128)}, u32[]{:S(2)}) copy-start(f32[16,1024]{0,1:T(8,128)} %get-tuple-element.16) | copy-start | bytes 196612
  280.1 99.0 %all-to-all-start = ((bf16[16,256,1024]{1,0,2:T(8,128)(2,1)}), bf16[16,256,1024]{1,0,2:T(8,128)(2,1)}, u32[]{:S(2)}, u32[]{:S(2)}) async-start(bf16[16,256,1024]{1,0,2:T(8,128)(2,1)} %divide_convert_fusion.2), calls=%async_computation | async-start | bytes 16777216 | tf_op jit(solution)/shard_map/all_to_all | solution.py:39
  309.0 75.1 %copy-start.4 = (f32[256,16]{0,1:T(8,128)S(1)}, f32[256,16]{0,1:T(8,128)}, u32[]{:S(2)}) copy-start(f32[256,16]{0,1:T(8,128)} %param.14) | copy-start | bytes 49156
  309.0 75.1 %copy-start.5 = (f32[256]{0:T(256)S(1)}, f32[256]{0:T(256)}, u32[]{:S(2)}) copy-start(f32[256]{0:T(256)} %param.15) | copy-start | bytes 3076
  379.1 143.3 %all-to-all-start.2 = ((bf16[16,1024,256]{2,0,1:T(8,128)(2,1)}), bf16[16,1024,256]{2,0,1:T(8,128)(2,1)}, u32[]{:S(2)}, u32[]{:S(2)}) async-start(bf16[16,1024,256]{2,0,1:T(8,128)(2,1)} %divide_convert_fusion), calls=%async_computation.2 | async-start | bytes 16777216 | tf_op jit(solution)/shard_map/all_to_all | solution.py:42
Sparse Core Ops, SparseCore 0:
  106.0 61.7 all-reduce.2
where the time goes:
time: 557 us; the launch traced here: 555 us
  waiting for transfers between devices  214 us (38%)
  local copies, waits for them, and re-layouts  112 us (20%)
  blocking collectives  112 us (20%)
  other arithmetic  87.4 us (16%)
  starting transfers between devices  15.3 us (3%)
  between operations  14.1 us (3%)
    all_gather x1, blocking collectives, on_device(): row_router = lax.all_gather(part_router, 'zero', axis=0, tiled=True)  97.2 us
    all_to_all x1, waiting for transfers between devices, on_device(): lax.all_to_all(narrow_up, 'zero', split_axis=2, concat_axis=1, tiled=True)  82 us
    all_to_all x1, waiting for transfers between devices, on_device(): lax.all_to_all(narrow_gate, 'zero', split_axis=2, concat_axis=1, tiled=True)  70 us
    unnamed x20, local copies, waits for them, and re-layouts  62.9 us
    psum x1, waiting for transfers between devices, on_device(): lax.psum((jnp.sum(jnp.abs(merged_gate), axis=1), jnp.sum(jnp.abs(merged_u...  62 us
    reduce_sum x1, other arithmetic, on_device(): jnp.sum(jnp.abs(merged_down), axis=2)  25.3 us
    all_to_all x2, local copies, waits for them, and re-layouts, on_device(): lax.all_to_all(narrow_down, 'zero', split_axis=1, concat_axis=2, tiled=True)  24.8 us
    convert_element_type x1, other arithmetic, on_device(): (merged_down / jnp.expand_dims(scale_down, 2)).astype(jnp.bfloat16)  23.8 us
  transfers between devices with their start and end apart: 4, of which 3 were waited for; matrix products, arithmetic and copies ran while one was open for 11% of the time, Pallas kernels for 0%

commit v1 on v0

--- a/solution.py
+++ b/solution.py
@@ -51,7 +51,8 @@
     )
     part_router = (router_weight * router_gain[:, None]).astype(jnp.bfloat16)
     row_router = lax.all_gather(part_router, "zero", axis=0, tiled=True)
-    serve_router = lax.all_gather(row_router, "bank", axis=1, tiled=True)
+    pieces = lax.all_gather(row_router, "bank", axis=0, tiled=False)
+    serve_router = jnp.concatenate(pieces, axis=1)
     return (final_gate, final_up, final_down, scale_gate, scale_up, scale_down, serve_router)
 
 

time: 557 us -> 557 us (level)
    unnamed x20 -> x19, local copies, waits for them, and re-layouts: 62.9 us -> 62.2 us
where the time goes in v1:
time: 557 us; the launch traced here: 555 us
  waiting for transfers between devices  214 us (38%)
  local copies, waits for them, and re-layouts  112 us (20%)
  blocking collectives  112 us (20%)
  other arithmetic  87.4 us (16%)
  starting transfers between devices  15.3 us (3%)
  between operations  14.1 us (3%)
    all_gather x1, blocking collectives, on_device(): row_router = lax.all_gather(part_router, 'zero', axis=0, tiled=True)  97.2 us
    all_to_all x1, waiting for transfers between devices, on_device(): lax.all_to_all(narrow_up, 'zero', split_axis=2, concat_axis=1, tiled=True)  82 us
    all_to_all x1, waiting for transfers between devices, on_device(): lax.all_to_all(narrow_gate, 'zero', split_axis=2, concat_axis=1, tiled=True)  70 us
    unnamed x19, local copies, waits for them, and re-layouts  62.2 us
    psum x1, waiting for transfers between devices, on_device(): lax.psum((jnp.sum(jnp.abs(merged_gate), axis=1), jnp.sum(jnp.abs(merged_u...  62 us
    reduce_sum x1, other arithmetic, on_device(): jnp.sum(jnp.abs(merged_down), axis=2)  25.3 us
    all_to_all x2, local copies, waits for them, and re-layouts, on_device(): lax.all_to_all(narrow_down, 'zero', split_axis=1, concat_axis=2, tiled=True)  24.8 us
    convert_element_type x1, other arithmetic, on_device(): (merged_down / jnp.expand_dims(scale_down, 2)).astype(jnp.bfloat16)  23.8 us
  transfers between devices with their start and end apart: 4, of which 3 were waited for; matrix products, arithmetic and copies ran while one was open for 11% of the time, Pallas kernels for 0%

profile of v1, /device:TPU:0, one launch (start us, length us, event | category | flops | bytes accessed | tf_op | source)
XLA Modules:
  0.0 554.7 jit_solution(2122364816939443716)
XLA Ops:
  7.2 0.0 all-reduce.3.cloned.1.call-start
  7.2 17.6 %copy.33 = f32[16,256,1024]{1,0,2:T(8,128)} copy(f32[16,256,1024]{2,1,0:T(8,128)} %param.8) | data formatting | bytes 33554432 | tf_op args[0]
  24.8 17.6 %copy.36 = f32[16,256,1024]{1,0,2:T(8,128)} copy(f32[16,256,1024]{2,1,0:T(8,128)} %param.10) | data formatting | bytes 33554432 | tf_op args[2]
  42.4 12.5 %copy.32 = bf16[16,256,1024]{1,0,2:T(8,128)(2,1)} copy(bf16[16,256,1024]{2,1,0:T(8,128)(2,1)} %param.9) | data formatting | bytes 16777216 | tf_op args[1]
  54.9 12.5 %copy.35 = bf16[16,256,1024]{1,0,2:T(8,128)(2,1)} copy(bf16[16,256,1024]{2,1,0:T(8,128)(2,1)} %param.11) | data formatting | bytes 16777216 | tf_op args[3]
  67.4 0.0 copy-start
  67.4 0.0 copy-start.1
  67.4 25.3 %abs_reduce_fusion = f32[16,1024]{0,1:T(8,128)} fusion(f32[16,1024,256]{2,1,0:T(8,128)} %param.12, bf16[16,1024,256]{2,1,0:T(8,128)(2,1)} %param.13), kind=kLoop, calls=%fused_computation.2 | loop fusion | flops 16760832 | bytes 25231360 | tf_op jit(solution)/shard_map/reduce_sum | solution.py:26
  92.7 0.0 copy-done
  92.7 0.0 copy-done.1
  92.7 13.2 %abs_reduce_fusion.1 = (f32[16,1024]{0,1:T(8,128)}, f32[16,1024]{0,1:T(8,128)}) fusion(f32[16,256,1024]{1,0,2:T(8,128)} %copy.36, bf16[16,256,1024]{1,0,2:T(8,128)(2,1)S(1)} %copy-done.1, f32[16,256,1024]{1,0,2:T(8,128)} %copy.33, bf16[16,256,1024]{1,0,2:T(8,128)(2,1)S(1)} %copy-done), kind=kLoop, calls=%fused_computation.4 | loop fusion | flops 33521664 | bytes 50462720 | tf_op jit(solution)/shard_map/reduce_sum | solution.py:25
  105.9 0.0 all-reduce.3.cloned.1.call-update
  105.9 62.0 %all-reduce.3.cloned.1.call-done = (f32[16,1024]{0,1:T(8,128)}, f32[16,1024]{0,1:T(8,128)}, f32[16,1024]{0,1:T(8,128)}) async-done(((f32[16,1024]{0,1:T(8,128)}, f32[16,1024]{0,1:T(8,128)}, f32[16,1024]{0,1:T(8,128)}), (f32[16,1024]{0,1:T(8,128)}, f32[16,1024]{0,1:T(8,128)}, f32[16,1024]{0,1:T(8,128)})) %all-reduce.3.cloned.1.call-update) | async-done | bytes 196624 | tf_op jit(solution)/shard_map/psum | solution.py:22
  167.9 1.1 broadcast_multiply_fusion.1
  169.0 12.0 %divide_convert_fusion.1 = bf16[16,256,1024]{1,0,2:T(8,128)(2,1)} fusion(f32[16,256,1024]{1,0,2:T(8,128)} %copy.36, bf16[16,256,1024]{1,0,2:T(8,128)(2,1)} %copy.35, f32[16,1024]{0,1:T(8,128)S(1)} %broadcast_multiply_fusion.1), kind=kLoop, calls=%fused_computation.3 | loop fusion | flops 16777216 | bytes 33619968 | tf_op jit(solution)/shard_map/convert_element_type | solution.py:35
  180.9 0.0 copy-start.3
  180.9 5.1 all-to-all-start.1
  186.0 0.0 copy-done.3
  186.1 12.0 %divide_convert_fusion.2 = bf16[16,256,1024]{1,0,2:T(8,128)(2,1)} fusion(f32[16,256,1024]{1,0,2:T(8,128)} %copy.33, bf16[16,256,1024]{1,0,2:T(8,128)(2,1)} %copy.32, f32[16,1024]{0,1:T(8,128)S(1)} %broadcast_multiply_fusion.2), kind=kLoop, calls=%fused_computation.6 | loop fusion | flops 16777216 | bytes 33619968 | tf_op jit(solution)/shard_map/convert_element_type | solution.py:34
  198.1 0.0 copy-start.2
  198.1 82.0 %all-to-all-done.1 = bf16[16,256,1024]{1,0,2:T(8,128)(2,1)} async-done(((bf16[16,256,1024]{1,0,2:T(8,128)(2,1)}), bf16[16,256,1024]{1,0,2:T(8,128)(2,1)}, u32[]{:S(2)}, u32[]{:S(2)}) %all-to-all-start.1) | async-done | bytes 8388640 | tf_op jit(solution)/shard_map/all_to_all | solution.py:40
  280.1 5.1 all-to-all-start
  285.2 0.0 copy-done.2
  285.3 23.8 %divide_convert_fusion = bf16[16,1024,256]{2,0,1:T(8,128)(2,1)} fusion(f32[16,1024,256]{2,1,0:T(8,128)} %param.12, f32[16,1024]{0,1:T(8,128)S(1)} %broadcast_multiply_fusion, bf16[16,1024,256]{2,1,0:T(8,128)(2,1)} %param.13), kind=kLoop, calls=%fused_computation.1 | loop fusion | flops 16777216 | bytes 33619968 | tf_op jit(solution)/shard_map/convert_element_type | solution.py:36
  309.0 0.0 copy-start.4
  309.0 0.0 copy-start.5
  309.0 70.0 %all-to-all-done = bf16[16,256,1024]{1,0,2:T(8,128)(2,1)} async-done(((bf16[16,256,1024]{1,0,2:T(8,128)(2,1)}), bf16[16,256,1024]{1,0,2:T(8,128)(2,1)}, u32[]{:S(2)}, u32[]{:S(2)}) %all-to-all-start) | async-done | bytes 8388640 | tf_op jit(solution)/shard_map/all_to_all | solution.py:39
  379.1 5.0 all-to-all-start.2
  384.1 0.0 copy-done.4
  384.1 0.0 copy-done.5
  384.1 97.2 %all_gather.9 = bf16[2048,16]{0,1:T(8,128)(2,1)S(1)} all-gather(bf16[256,16]{0,1:T(8,128)(2,1)S(1)} %multiply_convert_fusion), channel_id=1, replica_groups=mesh['bank'=4,'zero'=8] {'zero'}, dimensions={0}, use_global_device_ids=true | all-gather | bytes 73728 | tf_op jit(solution)/shard_map/all_gather | solution.py:53
  481.3 14.4 %all-gather = bf16[8192,16]{0,1:T(8,128)(2,1)S(1)} all-gather(bf16[2048,16]{0,1:T(8,128)(2,1)S(1)} %all_gather.9), channel_id=2, replica_groups=mesh['bank'=4,'zero'=8] {'bank'}, dimensions={0}, use_global_device_ids=true | all-gather | bytes 327680 | tf_op jit(solution)/shard_map/all_gather | solution.py:54
  495.7 0.7 copy.54
  496.5 0.7 copy.42
  497.1 0.7 copy.43
  497.8 0.7 copy.44
  498.5 12.3 %copy.37 = bf16[16,8,256,128]{3,2,1,0:T(8,128)(2,1)} copy(bf16[16,8,256,128]{2,0,3,1:T(8,128)(2,1)} %bitcast.4) | data formatting | bytes 16777216 | tf_op jit(solution)/shard_map/all_to_all | solution.py:40
  510.8 12.3 %copy.34 = bf16[16,8,256,128]{3,2,1,0:T(8,128)(2,1)} copy(bf16[16,8,256,128]{2,0,3,1:T(8,128)(2,1)} %bitcast.1) | data formatting | bytes 16777216 | tf_op jit(solution)/shard_map/all_to_all | solution.py:39
  523.0 0.0 all-to-all-done.2
  523.0 11.4 %copy.40 = bf16[16,128,8,256]{3,2,1,0:T(8,128)(2,1)} copy(bf16[16,128,8,256]{3,0,1,2:T(8,128)(2,1)} %bitcast.7) | data formatting | bytes 16777216 | tf_op jit(solution)/shard_map/all_to_all | solution.py:42
  534.4 13.4 %all_to_all.50 = bf16[16,128,2048]{2,1,0:T(8,128)(2,1)} reshape(bf16[16,128,8,256]{3,2,1,0:T(8,128)(2,1)} %copy.40) | data formatting | bytes 16777216 | tf_op jit(solution)/shard_map/all_to_all | solution.py:42
  (6 shorter events, 0.1 us)
Async XLA Ops:
  7.2 160.7 %all-reduce.3.cloned.1.call-start = ((), (), s32[]{:S(2)}) async-start(), calls=%async_computation.3 | async-start | bytes 3145728 | tf_op jit(solution)/shard_map/psum | solution.py:22
  67.4 25.3 %copy-start = (bf16[16,256,1024]{1,0,2:T(8,128)(2,1)S(1)}, bf16[16,256,1024]{1,0,2:T(8,128)(2,1)}, u32[]{:S(2)}) copy-start(bf16[16,256,1024]{1,0,2:T(8,128)(2,1)} %copy.32) | copy-start | bytes 25165828
  67.4 25.3 %copy-start.1 = (bf16[16,256,1024]{1,0,2:T(8,128)(2,1)S(1)}, bf16[16,256,1024]{1,0,2:T(8,128)(2,1)}, u32[]{:S(2)}) copy-start(bf16[16,256,1024]{1,0,2:T(8,128)(2,1)} %copy.35) | copy-start | bytes 25165828
  180.9 5.1 copy-start.3
  180.9 99.1 %all-to-all-start.1 = ((bf16[16,256,1024]{1,0,2:T(8,128)(2,1)}), bf16[16,256,1024]{1,0,2:T(8,128)(2,1)}, u32[]{:S(2)}, u32[]{:S(2)}) async-start(bf16[16,256,1024]{1,0,2:T(8,128)(2,1)} %divide_convert_fusion.1), calls=%async_computation.1 | async-start | bytes 16777216 | tf_op jit(solution)/shard_map/all_to_all | solution.py:40
  198.1 87.1 %copy-start.2 = (f32[16,1024]{0,1:T(8,128)S(1)}, f32[16,1024]{0,1:T(8,128)}, u32[]{:S(2)}) copy-start(f32[16,1024]{0,1:T(8,128)} %get-tuple-element.16) | copy-start | bytes 196612
  280.1 99.0 %all-to-all-start = ((bf16[16,256,1024]{1,0,2:T(8,128)(2,1)}), bf16[16,256,1024]{1,0,2:T(8,128)(2,1)}, u32[]{:S(2)}, u32[]{:S(2)}) async-start(bf16[16,256,1024]{1,0,2:T(8,128)(2,1)} %divide_convert_fusion.2), calls=%async_computation | async-start | bytes 16777216 | tf_op jit(solution)/shard_map/all_to_all | solution.py:39
  309.0 75.1 %copy-start.4 = (f32[256,16]{0,1:T(8,128)S(1)}, f32[256,16]{0,1:T(8,128)}, u32[]{:S(2)}) copy-start(f32[256,16]{0,1:T(8,128)} %param.14) | copy-start | bytes 49156
  309.0 75.1 %copy-start.5 = (f32[256]{0:T(256)S(1)}, f32[256]{0:T(256)}, u32[]{:S(2)}) copy-start(f32[256]{0:T(256)} %param.15) | copy-start | bytes 3076
  379.1 144.0 %all-to-all-start.2 = ((bf16[16,1024,256]{2,0,1:T(8,128)(2,1)}), bf16[16,1024,256]{2,0,1:T(8,128)(2,1)}, u32[]{:S(2)}, u32[]{:S(2)}) async-start(bf16[16,1024,256]{2,0,1:T(8,128)(2,1)} %divide_convert_fusion), calls=%async_computation.2 | async-start | bytes 16777216 | tf_op jit(solution)/shard_map/all_to_all | solution.py:42
Sparse Core Ops, SparseCore 0:
  106.0 61.7 all-reduce.2
